TPU v7x, 32 devices: a whole 2x2x4 slice. The times are simulated.
32 devices in a mesh: expert: 4 (over y, core), tensor: 8 (over z, x).
Axes of the slice: x: 2, y: 2, z: 4, core: 2. Of those that a mesh axis runs over, the one named last changes fastest.
Arguments:
- tokens: bfloat16 [1024, 6144], P('expert'), may hold values from -6 to 6
- expert_ids: int32 [1024, 2], P('expert'), may hold values from 0 to 3, all different within a row; in each aligned block of 256 rows (0 to 255, 256 to 511, ...) at most 192 rows name the same one
- gate_weights: float32 [1024, 2], P('expert'), may hold values from 0.2 to 1
- w_gate: bfloat16 [4, 6144, 16384], P('expert', None, 'tensor'), may hold values from -0.078125 to 0.078125
- w_up: bfloat16 [4, 6144, 16384], P('expert', None, 'tensor'), may hold values from -0.078125 to 0.078125
- w_down: bfloat16 [4, 16384, 6144], P('expert', 'tensor'), may hold values from -0.0625 to 0.0625
Outputs:
- mixed: bfloat16 [1024, 6144], P(('expert', 'tensor'))
Inputs may be any that keep to these rules, and one draw needn't show every extreme that they name: `expert_ids`: each token names two different experts. Among the 256 tokens held at one index along `expert`, no expert is named by more than 192 tokens, and in some such blocks one expert is named by exactly 192.
All inputs are finite; a program needn't handle non-finite values.
Results may differ from a plain program's by a relative error of at most 0.005.
Values may be sent and summed in bfloat16 or wider, within the bound.
A program may use at most 192 MiB of HBM per device.

v0:
```python
import jax
import jax.numpy as jnp
from jax import lax
from jax.sharding import PartitionSpec as P


def body(tokens, expert_ids, gate_weights, w_gate, w_up, w_down):
    tok_rows = tokens.shape[0]
    width = tokens.shape[1]
    groups = lax.axis_size("expert")
    capacity = 3 * tok_rows // 4
    slot_count = groups * capacity
    pair_hot = (
        expert_ids[:, :, None] == jnp.arange(groups, dtype=jnp.int32)[None, None, :]
    ).astype(jnp.int32)
    flat_hot = pair_hot.reshape(2 * tok_rows, groups)
    earlier = jnp.cumsum(flat_hot, axis=0) - flat_hot
    slot_rank = jnp.sum(earlier * flat_hot, axis=1)
    slot_index = expert_ids.reshape(-1) * capacity + slot_rank
    matched = (slot_index[None, :] == jnp.arange(slot_count, dtype=jnp.int32)[:, None]).astype(
        jnp.int32
    )
    matched = matched.reshape(slot_count, tok_rows, 2)
    taken = jnp.sum(matched, axis=2)
    slot_token = jnp.sum(taken * jnp.arange(tok_rows, dtype=jnp.int32)[None, :], axis=1)
    filled = jnp.sum(taken, axis=1) > 0
    combine = jnp.sum(matched.astype(jnp.float32) * gate_weights[None, :, :], axis=2)
    outgoing = jnp.where(filled[:, None], tokens[slot_token], jnp.zeros((), jnp.bfloat16))
    outgoing = outgoing.reshape(groups, capacity, width)
    arrived = lax.all_to_all(outgoing, "expert", split_axis=0, concat_axis=0, tiled=True)
    inputs = arrived.reshape(slot_count, width)
    gate_proj = jnp.dot(inputs, w_gate[0], preferred_element_type=jnp.float32)
    up_proj = jnp.dot(inputs, w_up[0], preferred_element_type=jnp.float32)
    hidden = (jax.nn.silu(gate_proj) * up_proj).astype(jnp.bfloat16)
    down_local = w_down[0]
    partial_value = lax.dot_general(
        down_local, hidden, (((0,), (1,)), ((), ())), preferred_element_type=jnp.float32
    )
    returned = lax.all_to_all(partial_value, "expert", split_axis=1, concat_axis=1, tiled=True)
    mixed_part = jnp.dot(returned, combine, precision=lax.Precision.HIGHEST)
    summed = lax.psum_scatter(mixed_part, "tensor", scatter_dimension=1, tiled=True)
    return summed.T.astype(jnp.bfloat16)


def solution(mesh):
    placed = (
        P("expert", None),
        P("expert", None),
        P("expert", None),
        P("expert", None, "tensor"),
        P("expert", None, "tensor"),
        P("expert", "tensor", None),
    )
    return jax.shard_map(
        body, mesh=mesh, in_specs=placed, out_specs=P(("expert", "tensor"), None), check_vma=False
    )
```

profile of v0, /device:TPU:0, one launch (start us, length us, event | category | flops | bytes accessed | tf_op | source)
XLA Modules:
  0.0 570.6 jit_solution(1858369969009648385)
XLA Ops:
  6.5 0.0 copy-start
  6.5 1.0 copy.19
  7.5 0.1 eq.44
  7.6 0.1 eq.40
  7.8 1.2 reduce-window.6
  9.0 0.2 slice_reduce_fusion
  9.2 0.2 reduce-window.9
  9.4 0.1 add_bitcast_fusion
  9.5 0.1 reduce_sum.50
  9.7 0.1 copy.21
  9.8 0.7 multiply_add_fusion
  10.5 0.2 convert_reduce_fusion.1
  10.7 0.2 multiply_reduce_fusion
  10.9 0.1 copy-done.2
  11.1 0.1 gt.11
  11.2 0.0 copy-done
  11.2 8.0 %gather_fusion = bf16[768,6144]{1,0:T(8,128)(2,1)} fusion(bf16[256,6144]{1,0:T(8,128)(2,1)S(1)} %copy-done, s32[1024]{0:T(1024)S(1)} %pad_clamp_fusion), kind=kCustom, calls=%fused_computation | custom fusion | bytes 18877440 | tf_op jit(solution)/shard_map/gather | solution.py:28
  19.2 8.1 %broadcast_select_fusion = bf16[4,192,6144]{2,1,0:T(8,128)(2,1)} fusion(bf16[4,192,6144]{2,1,0:T(8,128)(2,1)} %bitcast.43, pred[4,192]{1,0:T(4,128)(4,1)S(1)} %gt.11), kind=kLoop, calls=%fused_computation.7 | loop fusion | flops 4718592 | bytes 18875136 | tf_op jit(solution)/shard_map/jit(_where)/select_n | solution.py:28
  27.3 109.4 %all_to_all.17 = bf16[4,192,6144]{2,1,0:T(8,128)(2,1)S(1)} all-to-all(bf16[4,192,6144]{2,1,0:T(8,128)(2,1)} %broadcast_select_fusion), channel_id=1, replica_groups=mesh['expert'=4,'tensor'=8] {'expert'}, dimensions={0} | all-to-all | bytes 18874368 | tf_op jit(solution)/shard_map/all_to_all | solution.py:30
  136.6 23.2 %fusion.4 = f32[768,2048]{1,0:T(8,128)S(1)} fusion(bf16[768,6144]{1,0:T(8,128)(2,1)S(1)} %bitcast.45, bf16[1,6144,2048]{2,1,0:T(8,128)(2,1)} %param.9), kind=kOutput, calls=%fused_computation.5 | convolution fusion | flops 19327352832 | bytes 40894464 | tf_op jit(solution)/shard_map/dot_general | solution.py:32
  159.8 23.8 %multiply_convert_fusion = bf16[768,2048]{1,0:T(8,128)(2,1)S(1)} fusion(f32[768,2048]{1,0:T(8,128)S(1)} %fusion.4, bf16[768,6144]{1,0:T(8,128)(2,1)S(1)} %bitcast.46, bf16[1,6144,2048]{2,1,0:T(8,128)(2,1)} %param.10), kind=kOutput, calls=%fused_computation.8 | convolution fusion | flops 19336790016 | bytes 44040192 | tf_op jit(solution)/shard_map/dot_general | solution.py:33
  183.6 25.1 %fusion = f32[768,6144]{1,0:T(8,128)} fusion(bf16[768,2048]{1,0:T(8,128)(2,1)S(1)} %multiply_convert_fusion, bf16[1,2048,6144]{2,1,0:T(8,128)(2,1)} %param.11), kind=kOutput, calls=%fused_computation.1 | convolution fusion | flops 19327352832 | bytes 47185920 | tf_op jit(solution)/shard_map/dot_general | solution.py:36
  208.7 7.5 %all-to-all-start.1 = ((f32[6144,4,192]{0,2,1:T(8,128)}), f32[6144,4,192]{0,2,1:T(8,128)}, u32[]{:S(2)}, u32[]{:S(2)}) async-start(f32[6144,4,192]{0,2,1:T(8,128)} %bitcast.44), calls=%async_computation.1 | async-start | bytes 37748736 | tf_op jit(solution)/shard_map/all_to_all | solution.py:39
  216.2 0.3 reduce-scatter.2.cloned.1.call-start
  216.5 0.0 copy-done.3
  216.5 0.0 copy-done.4
  216.5 1.2 fusion.9
  217.7 204.0 %all-to-all-done.1 = f32[6144,4,192]{0,2,1:T(8,128)} async-done(((f32[6144,4,192]{0,2,1:T(8,128)}), f32[6144,4,192]{0,2,1:T(8,128)}, u32[]{:S(2)}, u32[]{:S(2)}) %all-to-all-start.1) | async-done | bytes 18874400 | tf_op jit(solution)/shard_map/all_to_all | solution.py:39
  421.7 21.1 %fusion.15 = f32[6144,256]{0,1:T(8,128)} fusion(f32[6144,768]{0,1:T(8,128)} %bitcast.8, f32[768,256]{1,0:T(8,128)} %fusion.9), kind=kOutput, calls=%fused_computation.31 | convolution fusion | flops 14495514624 | bytes 25952256 | tf_op jit(solution)/shard_map/dot_general | solution.py:40
  442.8 0.0 reduce-scatter.2.cloned.1.call-update
  442.8 119.1 %reduce-scatter.2.cloned.1.call-done = f32[6144,32]{0,1:T(8,128)} async-done(((f32[6144,256]{0,1:T(8,128)}), f32[6144,32]{0,1:T(8,128)}) %reduce-scatter.2.cloned.1.call-update) | async-done | bytes 786448 | tf_op jit(solution)/shard_map/reduce_scatter | solution.py:41
  561.9 1.9 convert_bitcast_fusion
  (10 shorter events, 0.1 us)
Async XLA Ops:
  6.5 4.6 copy-start
  10.5 0.6 copy-start.2
  208.7 7.8 %copy-start.3 = (s32[256,2]{0,1:T(2,128)S(1)}, s32[256,2]{0,1:T(2,128)}, u32[]{:S(2)}) copy-start(s32[256,2]{0,1:T(2,128)} %copy-done.2) | copy-start | bytes 6148
  208.7 7.8 %copy-start.4 = (f32[256,2]{0,1:T(2,128)S(1)}, f32[256,2]{0,1:T(2,128)}, u32[]{:S(2)}) copy-start(f32[256,2]{0,1:T(2,128)} %param.8) | copy-start | bytes 6148
  208.7 213.0 %all-to-all-start.1 = ((f32[6144,4,192]{0,2,1:T(8,128)}), f32[6144,4,192]{0,2,1:T(8,128)}, u32[]{:S(2)}, u32[]{:S(2)}) async-start(f32[6144,4,192]{0,2,1:T(8,128)} %bitcast.44), calls=%async_computation.1 | async-start | bytes 37748736 | tf_op jit(solution)/shard_map/all_to_all | solution.py:39
  216.2 345.7 %reduce-scatter.2.cloned.1.call-start = ((), (), s32[]{:S(2)}) async-start(), calls=%async_computation.3 | async-start | bytes 7077888 | tf_op jit(solution)/shard_map/reduce_scatter | solution.py:41
  421.7 142.1 %copy-start.1 = (bf16[256,6144]{1,0:T(8,128)(2,1)S(1)}, bf16[256,6144]{1,0:T(8,128)(2,1)}, u32[]{:S(2)}) copy-start(bf16[256,6144]{1,0:T(8,128)(2,1)} %param.6) | copy-start | bytes 9437188
Sparse Core Ops, SparseCore 0:
  442.9 118.9 reduce-scatter.1
where the time goes:
time: 571 us
  waiting for transfers between devices  323 us (57%)
  blocking collectives  109 us (19%)
  matrix products  93.1 us (16%)
  other arithmetic  13.9 us (2%)
  between operations  13.5 us (2%)
  local copies, waits for them, and re-layouts  9.94 us (2%)
  starting transfers between devices  7.73 us (1%)
    all_to_all x1, waiting for transfers between devices, body(): lax.all_to_all(partial_value, 'expert', split_axis=1, concat_axis=1, tile...  204 us
    reduce_scatter x1, waiting for transfers between devices, body(): lax.psum_scatter(mixed_part, 'tensor', scatter_dimension=1, tiled=True)  119 us
    all_to_all x1, blocking collectives, body(): lax.all_to_all(outgoing, 'expert', split_axis=0, concat_axis=0, tiled=True)  109 us
    dot_general x1, matrix products, body(): lax.dot_general(down_local, hidden, (((0,), (1,)), ((), ())), preferred_e...  25.1 us
    dot_general x1, matrix products, body(): up_proj = jnp.dot(inputs, w_up[0], preferred_element_type=jnp.float32)  23.8 us
    dot_general x1, matrix products, body(): gate_proj = jnp.dot(inputs, w_gate[0], preferred_element_type=jnp.float32)  23.2 us
    dot_general x1, matrix products, body(): mixed_part = jnp.dot(returned, combine, precision=lax.Precision.HIGHEST)  21.1 us
  transfers between devices with their start and end apart: 2, of which 2 were waited for; matrix products, arithmetic and copies ran while one was open for 0% of the time, Pallas kernels for 0%

commit v1 on v0

v1 whole, which is shorter than its diff:
```python
import jax
import jax.numpy as jnp
from jax import lax
from jax.sharding import PartitionSpec as P

AXES = ("expert", "tensor")
CHUNKS = 2


def body(tokens, expert_ids, gate_weights, w_gate, w_up, w_down):
    tok_rows, width = tokens.shape
    experts = lax.axis_size("expert")
    parts = lax.axis_size("tensor")
    owned = tok_rows // parts
    piece = owned // CHUNKS
    me = lax.axis_index("expert")
    part = lax.axis_index("tensor")

    hot = expert_ids[:, :, None] == jnp.arange(experts, dtype=jnp.int32)[None, None, :]
    weight = jnp.sum(jnp.where(hot, gate_weights[:, :, None], 0.0), axis=1)
    weight = lax.all_gather(weight.T, "expert", axis=0)
    weight = lax.dynamic_index_in_dim(weight, me, axis=1, keepdims=False)
    weight = weight.reshape(experts * parts, CHUNKS, piece)

    rows = lax.dynamic_slice_in_dim(tokens, part * owned, owned, axis=0)
    gathered = [
        lax.all_gather(rows[c * piece:(c + 1) * piece], AXES, axis=0, tiled=True)
        for c in range(CHUNKS)
    ]
    results = []
    for c in range(CHUNKS):
        inputs = gathered[c]
        gate_proj = jnp.dot(inputs, w_gate[0], preferred_element_type=jnp.float32)
        up_proj = jnp.dot(inputs, w_up[0], preferred_element_type=jnp.float32)
        hidden = (jax.nn.silu(gate_proj) * up_proj).astype(jnp.bfloat16)
        out = jnp.dot(hidden, w_down[0], preferred_element_type=jnp.float32)
        out = (out * weight[:, c].reshape(-1)[:, None]).astype(jnp.bfloat16)
        results.append(lax.psum_scatter(out, AXES, scatter_dimension=0, tiled=True))
    return jnp.concatenate(results, axis=0).astype(jnp.bfloat16)


def solution(mesh):
    placed = (
        P("expert", None),
        P("expert", None),
        P("expert", None),
        P("expert", None, "tensor"),
        P("expert", None, "tensor"),
        P("expert", "tensor", None),
    )
    return jax.shard_map(
        body, mesh=mesh, in_specs=placed, out_specs=P(AXES, None), check_vma=False
    )
```

time: 571 us -> 400 us (0.70)
  blocking collectives: 109 us -> 6.27 us
  waiting for transfers between devices: 323 us -> 247 us
  matrix products: 93.1 us -> 128 us
  other arithmetic: 13.9 us -> 2.5 us
  starting transfers between devices: 7.73 us -> 0.12 us
  local copies, waits for them, and re-layouts: 9.94 us -> 2.77 us
    all_to_all x1 -> x0, waiting for transfers between devices: 204 us -> none  [body(): lax.all_to_all(partial_value, 'expert', split_axis=1, concat_axis=1, tile...]
    all_to_all x1 -> x0, blocking collectives: 109 us -> none  [body(): lax.all_to_all(outgoing, 'expert', split_axis=0, concat_axis=0, tiled=True)]
    all_gather x0 -> x2, waiting for transfers between devices: none -> 71.7 us  [body(): lax.all_gather(rows[c * piece:(c + 1) * piece], AXES, axis=0, tiled=True)]
    reduce_scatter x1 -> x2, waiting for transfers between devices: 119 us -> 175 us  [body(): results.append(lax.psum_scatter(out, AXES, scatter_dimension=0, tiled=True))]
    dot_general x1 -> x2, matrix products: 23.2 us -> 48.8 us  [body(): gate_proj = jnp.dot(inputs, w_gate[0], preferred_element_type=jnp.float32)]
    dot_general x1 -> x2, matrix products: 23.8 us -> 38.3 us  [body(): up_proj = jnp.dot(inputs, w_up[0], preferred_element_type=jnp.float32)]
    select_n x2 -> x0, other arithmetic: 8.09 us -> none  [the longest x1 8.08 us: body(): jnp.where(filled[:, None], tokens[slot_token], jnp.zeros((), jnp.bfloat16))]
    gather x1 -> x0, local copies, waits for them, and re-layouts: 8.01 us -> none  [body(): tokens[slot_token]]
  transfers between devices with their start and end apart: 2 -> 4, of which waited for: 2 -> 4; matrix products, arithmetic and copies ran while one was open for 0% -> 32% of each run, Pallas kernels for 0% -> 0%
where the time goes in v1:
time: 400 us
  waiting for transfers between devices  247 us (62%)
  matrix products  128 us (32%)
  between operations  13.2 us (3%)
  blocking collectives  6.27 us (2%)
    reduce_scatter x2, waiting for transfers between devices, body(): results.append(lax.psum_scatter(out, AXES, scatter_dimension=0, tiled=True))  175 us
    all_gather x2, waiting for transfers between devices, body(): lax.all_gather(rows[c * piece:(c + 1) * piece], AXES, axis=0, tiled=True)  71.7 us
    dot_general x2, matrix products, body(): gate_proj = jnp.dot(inputs, w_gate[0], preferred_element_type=jnp.float32)  48.8 us
    dot_general x2, matrix products, body(): out = jnp.dot(hidden, w_down[0], preferred_element_type=jnp.float32)  40.6 us
    dot_general x2, matrix products, body(): up_proj = jnp.dot(inputs, w_up[0], preferred_element_type=jnp.float32)  38.3 us
  transfers between devices with their start and end apart: 4, of which 4 were waited for; matrix products, arithmetic and copies ran while one was open for 32% of the time, Pallas kernels for 0%

profile of v1, /device:TPU:0, one launch (start us, length us, event | category | flops | bytes accessed | tf_op | source)
XLA Modules:
  0.0 400.1 jit_solution(16893816836831131884)
XLA Ops:
  6.5 0.0 all-gather.5.cloned.1.call-start
  6.5 1.8 constant_dynamic-slice_fusion
  8.3 0.0 all-gather.5.cloned.1.call-update
  8.4 0.0 all-gather.7.cloned.1.call-start
  8.4 0.7 all-gather.7.cloned.1.call-update
  9.1 0.0 reduce-scatter.3.cloned.1.call-start
  9.2 0.7 select_reduce_fusion
  9.9 6.3 %all-gather.1 = f32[4,4,256]{2,1,0:T(4,128)S(1)} all-gather(f32[1,4,256]{2,1,0:T(4,128)S(1)} %bitcast.32), channel_id=2, replica_groups=mesh['expert'=4,'tensor'=8] {'expert'}, dimensions={0}, use_global_device_ids=true | all-gather | bytes 20480 | tf_op jit(solution)/shard_map/all_gather | solution.py:21
  16.2 0.1 reshape.8
  16.3 0.1 slice_reduce_fusion.1
  16.4 0.1 mul.39
  16.5 0.7 mul.44
  17.1 65.2 %all-gather.5.cloned.1.call-done = bf16[512,6144]{1,0:T(8,128)(2,1)} async-done(((bf16[16,6144]{1,0:T(8,128)(2,1)}), bf16[512,6144]{1,0:T(8,128)(2,1)}) %all-gather.5.cloned.1.call-update) | async-done | bytes 6291472 | tf_op jit(solution)/shard_map/all_gather | solution.py:27
  82.3 0.0 copy-start.2
  82.3 24.4 %fusion.10 = f32[512,2048]{1,0:T(8,128)} fusion(bf16[512,6144]{1,0:T(8,128)(2,1)} %all-gather.5.cloned.1.call-done, bf16[1,6144,2048]{2,1,0:T(8,128)(2,1)} %param.9), kind=kOutput, calls=%fused_computation.10 | convolution fusion | flops 12884901888 | bytes 35651584 | tf_op jit(solution)/shard_map/dot_general | solution.py:33
  106.8 0.0 copy-done.2
  106.8 19.1 %multiply_convert_fusion.3 = bf16[512,2048]{1,0:T(8,128)(2,1)S(1)} fusion(f32[512,2048]{1,0:T(8,128)} %fusion.10, bf16[512,6144]{1,0:T(8,128)(2,1)S(1)} %copy-done.2, bf16[1,6144,2048]{2,1,0:T(8,128)(2,1)} %param.10), kind=kOutput, calls=%fused_computation.15 | convolution fusion | flops 12891193344 | bytes 37748736 | tf_op jit(solution)/shard_map/dot_general | solution.py:34
  125.9 20.7 %multiply_convert_fusion.1 = bf16[512,6144]{1,0:T(8,128)(2,1)} fusion(bf16[512,2048]{1,0:T(8,128)(2,1)S(1)} %multiply_convert_fusion.3, bf16[1,2048,6144]{2,1,0:T(8,128)(2,1)} %param.11, f32[512]{0:T(512)S(1)} %mul.39), kind=kOutput, calls=%fused_computation.13 | convolution fusion | flops 12891193344 | bytes 33556480 | tf_op jit(solution)/shard_map/dot_general | solution.py:36
  146.6 0.0 reduce-scatter.3.cloned.1.call-update
  146.6 0.0 reduce-scatter.5.cloned.1.call-start
  146.7 6.5 %all-gather.7.cloned.1.call-done = bf16[512,6144]{1,0:T(8,128)(2,1)} async-done(((bf16[16,6144]{1,0:T(8,128)(2,1)}), bf16[512,6144]{1,0:T(8,128)(2,1)}) %all-gather.7.cloned.1.call-update) | async-done | bytes 6291472 | tf_op jit(solution)/shard_map/all_gather | solution.py:27
  153.2 0.0 copy-start.1
  153.2 24.4 %fusion.8 = f32[512,2048]{1,0:T(8,128)} fusion(bf16[512,6144]{1,0:T(8,128)(2,1)} %all-gather.7.cloned.1.call-done, bf16[1,6144,2048]{2,1,0:T(8,128)(2,1)} %param.9), kind=kOutput, calls=%fused_computation.8 | convolution fusion | flops 12884901888 | bytes 35651584 | tf_op jit(solution)/shard_map/dot_general | solution.py:33
  177.6 0.0 copy-done.1
  177.6 0.0 copy-start
  177.6 19.2 %multiply_convert_fusion.2 = bf16[512,2048]{1,0:T(8,128)(2,1)S(1)} fusion(f32[512,2048]{1,0:T(8,128)} %fusion.8, bf16[512,6144]{1,0:T(8,128)(2,1)S(1)} %copy-done.1, bf16[1,6144,2048]{2,1,0:T(8,128)(2,1)} %param.10), kind=kOutput, calls=%fused_computation.14 | convolution fusion | flops 12891193344 | bytes 37748736 | tf_op jit(solution)/shard_map/dot_general | solution.py:34
  196.8 0.0 copy-done
  196.8 19.9 %multiply_convert_fusion = bf16[512,6144]{1,0:T(8,128)(2,1)} fusion(bf16[512,2048]{1,0:T(8,128)(2,1)S(1)} %multiply_convert_fusion.2, bf16[1,2048,6144]{2,1,0:T(8,128)(2,1)} %param.11, f32[512]{0:T(512)S(1)} %copy-done), kind=kOutput, calls=%fused_computation.12 | convolution fusion | flops 12891193344 | bytes 33556480 | tf_op jit(solution)/shard_map/dot_general | solution.py:36
  216.7 0.0 reduce-scatter.5.cloned.1.call-update
  216.7 55.6 %reduce-scatter.3.cloned.1.call-done = bf16[16,6144]{1,0:T(8,128)(2,1)} async-done(((bf16[512,6144]{1,0:T(8,128)(2,1)}), bf16[16,6144]{1,0:T(8,128)(2,1)}) %reduce-scatter.3.cloned.1.call-update) | async-done | bytes 196624 | tf_op jit(solution)/shard_map/reduce_scatter | solution.py:38
  272.3 119.4 %reduce-scatter.5.cloned.1.call-done = bf16[16,6144]{1,0:T(8,128)(2,1)} async-done(((bf16[512,6144]{1,0:T(8,128)(2,1)}), bf16[16,6144]{1,0:T(8,128)(2,1)}) %reduce-scatter.5.cloned.1.call-update) | async-done | bytes 196624 | tf_op jit(solution)/shard_map/reduce_scatter | solution.py:38
  391.7 1.8 pad_maximum_fusion
  (1 shorter events, 0.0 us)
Async XLA Ops:
  6.5 75.8 %all-gather.5.cloned.1.call-start = ((), (), s32[]{:S(2)}) async-start(), calls=%async_computation.2 | async-start | bytes 6488064 | tf_op jit(solution)/shard_map/all_gather | solution.py:27
  8.4 144.8 %all-gather.7.cloned.1.call-start = ((), (), s32[]{:S(2)}) async-start(), calls=%async_computation.4 | async-start | bytes 6488064 | tf_op jit(solution)/shard_map/all_gather | solution.py:27
  9.1 263.2 %reduce-scatter.3.cloned.1.call-start = ((), (), s32[]{:S(2)}) async-start(), calls=%async_computation.3 | async-start | bytes 6488064 | tf_op jit(solution)/shard_map/reduce_scatter | solution.py:38
  82.3 24.4 %copy-start.2 = (bf16[512,6144]{1,0:T(8,128)(2,1)S(1)}, bf16[512,6144]{1,0:T(8,128)(2,1)}, u32[]{:S(2)}) copy-start(bf16[512,6144]{1,0:T(8,128)(2,1)} %all-gather.5.cloned.1.call-done) | copy-start | bytes 18874372
  146.6 245.1 %reduce-scatter.5.cloned.1.call-start = ((), (), s32[]{:S(2)}) async-start(), calls=%async_computation.5 | async-start | bytes 6488064 | tf_op jit(solution)/shard_map/reduce_scatter | solution.py:38
  153.2 24.4 %copy-start.1 = (bf16[512,6144]{1,0:T(8,128)(2,1)S(1)}, bf16[512,6144]{1,0:T(8,128)(2,1)}, u32[]{:S(2)}) copy-start(bf16[512,6144]{1,0:T(8,128)(2,1)} %all-gather.7.cloned.1.call-done) | copy-start | bytes 18874372
  177.6 19.2 %copy-start = (f32[512]{0:T(512)S(1)}, f32[512]{0:T(512)}, u32[]{:S(2)}) copy-start(f32[512]{0:T(512)} %mul.44) | copy-start | bytes 6148
Sparse Core Ops, SparseCore 0:
  10.3 71.9 all-gather.4
  85.3 67.7 all-gather.6
  158.8 113.4 reduce-scatter.2
  277.8 113.8 reduce-scatter.4
